TPU v7x, 256 devices: a whole 4x4x8 slice. The times are simulated.
256 devices in a mesh: tm: 64 (over y, z, core), series: 4 (over x).
Axes of the slice: x: 4, y: 4, z: 8, core: 2. Of those that a mesh axis runs over, the one named last changes fastest.
Arguments:
- samples: float32 [256, 1048576], P(None, ('tm', 'series')), may hold values from -6 to 6
- taps: float32 [8], replicated, may hold values from 0.1 to 1
Outputs:
- coarse: float32 [256, 4096], P('series', 'tm')
- checksums: float32 [8, 256], P(None, 'series')
All inputs are finite; a program needn't handle non-finite values.
Results may differ from a plain program's by a relative error of at most 0.0001.
Values sent between devices are 32-bit elements; how exact they have to be, the bound alone decides.
A program may use at most 64 MiB of HBM per device.

v0:
```python
import math

import jax
import jax.numpy as jnp
from jax import lax
from jax.sharding import Mesh
from jax.sharding import PartitionSpec as P

LEVELS = 8
TM_SERIES = ("tm_0", "tm_1", "tm_2", "series")
TM = ("tm_0", "tm_1", "tm_2")


def shifted(block, axis, distance):
    devices = range(lax.axis_size(axis))
    route = [(i - distance, i) for i in devices if i - distance in devices]
    return lax.ppermute(block, axis, route)


def by_axis(shard, axes):
    for axis in axes:
        shard = lax.psum(shard, axis)
    return shard


def toeplitz_table(kernel, block):
    row_index = lax.iota(jnp.int32, block + 8)[:, None]
    col_index = lax.iota(jnp.int32, block // 2)[None, :]
    offset_map = 2 * col_index + 9 - row_index
    table = jnp.zeros((block + 8, block // 2), jnp.float32)
    for tap in range(8):
        table = table + jnp.where(offset_map == tap, kernel[tap], 0.0)
    return table


def decimate(signal, history, kernel):
    rows_count, length = signal.shape
    block = length if length <= 512 else math.gcd(length, 512)
    blocks_count = length // block
    shaped = signal.reshape(rows_count, blocks_count, block)
    tails = jnp.concatenate([history[:, None, :], shaped[:, :-1, block - 8 :]], axis=1)
    extended = jnp.concatenate([tails, shaped], axis=2)
    table = toeplitz_table(kernel, block)
    result = jnp.einsum("rbi,io->rbo", extended, table, precision=lax.Precision.HIGHEST)
    return result.reshape(rows_count, length // 2)


def level_sums(pyramid, block_count, block_index):
    partials = []
    for layer in pyramid:
        local_len = layer.shape[1]
        global_len = local_len * block_count
        position = (block_index * local_len + lax.iota(jnp.int32, local_len)).astype(jnp.float32)
        weights_pos = 1.0 + 2.0 * position / (global_len - 1)
        partials.append(jnp.sum(layer * weights_pos, axis=1) / math.sqrt(global_len))
    return jnp.stack(partials)


def body(samples, taps):
    kernel = taps * (math.sqrt(2.0) / jnp.sum(taps))
    series_count = lax.axis_size("series")
    series_index = lax.axis_index("series")
    all_series = samples.shape[0]
    slab = all_series // series_count
    pyramid = []
    history = shifted(samples[:, -8:], TM_SERIES, 1)
    first = decimate(samples, history, kernel)
    signal = lax.all_to_all(first, "series", split_axis=0, concat_axis=1, tiled=True)
    pyramid.append(signal)
    remaining = LEVELS - 1
    rows_count = signal.shape[0]
    depth = 8 * 2**remaining
    prior = shifted(signal[:, -depth:], TM, 1)
    extended = jnp.concatenate([prior, signal], axis=1)
    zero_history = jnp.zeros((rows_count, 8), jnp.float32)
    for level in range(remaining):
        extended = decimate(extended, zero_history, kernel)
        pyramid.append(extended[:, depth >> level + 1 :])
    signal = pyramid[-1]
    own = level_sums(pyramid, lax.axis_size(TM), lax.axis_index(TM))
    spread = jnp.zeros((LEVELS, all_series), jnp.float32)
    spread = lax.dynamic_update_slice_in_dim(spread, own, series_index * slab, 1)
    totals = by_axis(spread, TM_SERIES)
    mine = lax.dynamic_slice_in_dim(totals, series_index * slab, slab, 1)
    return (signal, mine)


def solution(mesh):
    finer = Mesh(
        mesh.devices.reshape(4, 8, 2, mesh.shape["series"]), ("tm_0", "tm_1", "tm_2", "series")
    )
    return jax.shard_map(
        body,
        mesh=finer,
        in_specs=(P(None, TM_SERIES), P()),
        out_specs=(P("series", TM), P(None, "series")),
        check_vma=False,
    )
```

profile of v0, /device:TPU:1, one launch (start us, length us, event | category | flops | bytes accessed | tf_op | source)
XLA Modules:
  0.0 164.2 jit_solution(8855181293399845930)
XLA Ops:
  0.6 5.6 %copy.6 = f32[256,4096]{0,1:T(8,128)} copy(f32[256,4096]{1,0:T(8,128)} %param.2) | data formatting | bytes 8388608 | tf_op args[0]
  6.2 0.7 slice.70
  6.9 3.9 %collective-permute-start = (f32[256,8]{0,1:T(8,128)S(1)}, f32[256,8]{0,1:T(8,128)S(1)}, u32[]{:S(2)}, u32[]{:S(2)}) collective-permute-start(f32[256,8]{0,1:T(8,128)S(1)} %slice.70), channel_id=1, source_target_pairs={{0,1},{1,2},{2,3},{3,4},{4,5},{5,6},{6,7},{7,8},{8,9},{9,10},{10,1... | collective-permute-start | bytes 24584 | tf_op jit(solution)/shard_map/ppermute | solution.py:17
  10.9 0.5 multiply_add_fusion.13
  11.4 0.6 multiply_add_fusion.12
  12.0 0.6 multiply_add_fusion.6
  12.6 0.6 reduce_sum.81
  13.9 0.7 fusion.366
  14.5 0.5 multiply_add_fusion.11
  15.1 0.8 slice.71
  15.9 15.8 %fusion = f32[256,8,256]{2,0,1:T(8,128)S(1)} fusion(f32[256,8,512]{0,2,1:T(8,128)} %bitcast.79, f32[256,7,8]{0,2,1:T(8,128)S(1)} %slice.71, f32[256,1,8]{0,2,1:T(8,128)S(1)} %bitcast.89, f32[]{:T(128)} %bitcast.9, f32[]{:T(128)} %bitcast.8, f32[]{:T(128)} %bitcast.7, f32[]{:T(128)} %bitcast.6, f32[]{:T(128)} %bitcast.5, f32[]{:T(128)} %bitcast.4, f32[]{:T(128)} %bitcast.3, ...), kind=kOutput, calls=%fused_computation | convolution fusion | flops 3276881920 | bytes 6358048 | tf_op jit(solution)/shard_map/rbi,io->rbo/dot_general | solution.py:44
  31.7 1.2 copy.8
  32.9 1.5 all_to_all.14
  34.4 4.6 %all-to-all-start = ((f32[4,64,2048]{2,1,0:T(8,128)}), f32[4,64,2048]{2,1,0:T(8,128)S(1)}, u32[]{:S(2)}, u32[]{:S(2)}) async-start(f32[4,64,2048]{2,1,0:T(8,128)} %all_to_all.14), calls=%async_computation | async-start | bytes 4194304 | tf_op jit(solution)/shard_map/all_to_all | solution.py:68
  39.1 0.5 multiply_add_fusion.9
  39.6 0.6 multiply_add_fusion.5
  40.2 0.6 multiply_add_fusion.4
  40.8 0.6 multiply_add_fusion.3
  41.5 1.9 %select_add_fusion.4 = (f32[152,72]{1,0:T(8,128)S(1)}, f32[152,72]{1,0:T(8,128)S(1)}) fusion(f32[]{:T(128)} %bitcast.3, f32[]{:T(128)} %bitcast.2, s32[72]{0:T(128)S(1)} %multiply_add_fusion.10, f32[]{:T(128)} %bitcast.4), kind=kLoop, calls=%fused_computation.152 | loop fusion | flops 87552 | bytes 87852 | tf_op jit(solution)/shard_map/add | solution.py:32
  43.4 21.8 %all-to-all-done = f32[4,64,2048]{2,1,0:T(8,128)S(1)} async-done(((f32[4,64,2048]{2,1,0:T(8,128)}), f32[4,64,2048]{2,1,0:T(8,128)S(1)}, u32[]{:S(2)}, u32[]{:S(2)}) %all-to-all-start) | async-done | bytes 2097184 | tf_op jit(solution)/shard_map/all_to_all | solution.py:68
  65.4 4.8 %collective-permute-start.1 = (f32[64,1024]{1,0:T(8,128)S(1)}, f32[64,1024]{1,0:T(8,128)S(1)}, u32[]{:S(2)}, u32[]{:S(2)}) collective-permute-start(f32[64,1024]{1,0:T(8,128)S(1)} %slice.72), channel_id=1, source_target_pairs={{0,4},{4,8},{8,12},{12,16},{16,20},{20,24},{24,28},{28,32},{32,36}... | collective-permute-start | bytes 786440 | tf_op jit(solution)/shard_map/ppermute | solution.py:17
  70.1 0.5 multiply_add_fusion.8
  70.7 0.8 fusion.9
  71.5 1.7 %collective-permute-done.1 = f32[64,1024]{1,0:T(8,128)S(1)} collective-permute-done((f32[64,1024]{1,0:T(8,128)S(1)}, f32[64,1024]{1,0:T(8,128)S(1)}, u32[]{:S(2)}, u32[]{:S(2)}) %collective-permute-start.1) | collective-permute-done | bytes 262176 | tf_op jit(solution)/shard_map/ppermute | solution.py:17
  73.3 0.2 pad_maximum_fusion
  73.4 0.2 copy.26
  73.7 0.2 slice.73
  73.9 8.5 %fusion.6 = f32[64,18,256]{2,0,1:T(8,128)S(1)} fusion(f32[64,17,8]{2,0,1:T(8,128)S(1)} %slice.73, f32[64,18,512]{2,0,1:T(8,128)S(1)} %bitcast.82, f32[]{:T(128)} %bitcast.9, f32[]{:T(128)} %bitcast.8, f32[]{:T(128)} %bitcast.7, f32[]{:T(128)} %bitcast.6, f32[]{:T(128)} %bitcast.5, f32[]{:T(128)} %bitcast.4, f32[]{:T(128)} %bitcast.3, f32[]{:T(128)} %bitcast.2, ...), kind=kOutput, calls=%fused_computation.7 | convolution fusion | flops 1845242880 | bytes 3574816 | tf_op jit(solution)/shard_map/rbi,io->rbo/dot_general | solution.py:44
  82.4 1.9 %copy.12 = f32[64,18,256]{2,1,0:T(8,128)} copy(f32[64,18,256]{2,0,1:T(8,128)S(1)} %fusion.6) | data formatting | bytes 2359296 | tf_op jit(solution)/shard_map/rbi,io->rbo/dot_general | solution.py:44
  84.2 1.6 reshape_reshape.6
  85.8 0.7 copy.13
  86.7 7.0 %fusion.10 = f32[64,9,256]{2,0,1:T(8,128)S(1)} fusion(f32[64,8,8]{2,0,1:T(8,128)S(1)} %slice.74, f32[64,9,512]{2,0,1:T(8,128)S(1)} %copy.13, f32[]{:T(128)} %bitcast.9, f32[]{:T(128)} %bitcast.8, f32[]{:T(128)} %bitcast.7, f32[]{:T(128)} %bitcast.6, f32[]{:T(128)} %bitcast.5, f32[]{:T(128)} %bitcast.4, f32[]{:T(128)} %bitcast.3, f32[]{:T(128)} %bitcast.2, ...), kind=kOutput, calls=%fused_computation.16 | convolution fusion | flops 924218880 | bytes 1786912 | tf_op jit(solution)/shard_map/rbi,io->rbo/dot_general | solution.py:44
  93.8 5.9 %fusion.16 = f32[64,9,128]{2,0,1:T(8,128)S(1)} fusion(f32[64,8,8]{2,0,1:T(8,128)S(1)} %slice.75, f32[64,9,256]{2,0,1:T(8,128)S(1)} %fusion.10, f32[]{:T(128)} %bitcast.9, f32[]{:T(128)} %bitcast.8, f32[]{:T(128)} %bitcast.7, f32[]{:T(128)} %bitcast.6, f32[]{:T(128)} %bitcast.5, f32[]{:T(128)} %bitcast.4, f32[]{:T(128)} %bitcast.3, f32[]{:T(128)} %bitcast.2, ...), kind=kOutput, calls=%fused_computation.25 | convolution fusion | flops 234837504 | bytes 901664 | tf_op jit(solution)/shard_map/rbi,io->rbo/dot_general | solution.py:44
  99.9 5.7 %fusion.21 = f32[64,9,64]{2,0,1:T(8,128)S(1)} fusion(f32[64,8,8]{2,0,1:T(8,128)S(1)} %slice.76, f32[64,9,128]{2,0,1:T(8,128)S(1)} %fusion.16, f32[]{:T(128)} %bitcast.9, f32[]{:T(128)} %bitcast.8, f32[]{:T(128)} %bitcast.7, f32[]{:T(128)} %bitcast.6, f32[]{:T(128)} %bitcast.5, f32[]{:T(128)} %bitcast.4, f32[]{:T(128)} %bitcast.3, f32[]{:T(128)} %bitcast.2, ...), kind=kOutput, calls=%fused_computation.32 | convolution fusion | flops 60605952 | bytes 459040 | tf_op jit(solution)/shard_map/rbi,io->rbo/dot_general | solution.py:44
  105.7 0.2 copy.18
  106.1 0.2 fusion.15
  106.3 0.3 copy-done.2
  106.7 5.8 %fusion.70 = f32[64,9,32]{0,2,1:T(8,128)S(1)} fusion(f32[64,8,8]{2,0,1:T(8,128)S(1)} %slice.77, f32[64,9,64]{2,0,1:T(8,128)S(1)} %fusion.21, f32[]{:T(128)} %bitcast.9, f32[]{:T(128)} %bitcast.8, f32[]{:T(128)} %bitcast.7, f32[]{:T(128)} %bitcast.6, f32[]{:T(128)} %bitcast.5, f32[]{:T(128)} %bitcast.4, f32[]{:T(128)} %bitcast.3, f32[]{:T(128)} %bitcast.2, ...), kind=kOutput, calls=%fused_computation.80 | convolution fusion | flops 16104960 | bytes 237728 | tf_op jit(solution)/shard_map/rbi,io->rbo/dot_general | solution.py:44
  112.5 0.1 fusion.75
  112.8 5.5 %fusion.38 = f32[64,144]{1,0:T(8,128)S(1)} fusion(f32[]{:T(128)} %bitcast.9, f32[]{:T(128)} %bitcast.8, f32[]{:T(128)} %bitcast.7, f32[]{:T(128)} %bitcast.6, f32[]{:T(128)} %bitcast.5, f32[]{:T(128)} %bitcast.4, f32[]{:T(128)} %bitcast.3, f32[]{:T(128)} %bitcast.2, s32[144]{0:T(256)S(1)} %copy-done.7, f32[64,1,288]{0,2,1:T(8,128)S(1)} %bitcast.87), kind=kOutput, calls=%fused_computation.53 | convolution fusion | flops 33758208 | bytes 111200 | tf_op jit(solution)/shard_map/rbi,io->rbo/dot_general | solution.py:44
  118.4 0.2 fusion.218
  118.6 4.2 %multiply_reduce_fusion = (f32[64]{0:T(128)S(1)}, f32[64,64]{1,0:T(8,128)}) fusion(f32[64]{0:T(128)S(1)} %copy-done.10, f32[152,72]{1,0:T(8,128)S(1)} %get-tuple-element.11, f32[152,72]{1,0:T(8,128)S(1)} %get-tuple-element.10, pred[152,72]{1,0:T(8,128)(4,1)S(1)} %fusion.145, s32[152,72]{1,0:T(8,128)S(1)} %iota_subtract_fusion.3, f32[]{:T(128)} %bitcast.9, ...), kind=kOutput, calls=%fused_computation.222 | convolution fusion | flops 7625152 | bytes 196052 | tf_op jit(solution)/shard_map/rbi,io->rbo/dot_general | solution.py:44
  122.9 0.3 dynamic_update_slice.3
  123.2 8.8 %psum.28 = f32[8,256]{1,0:T(8,128)S(1)} all-reduce(f32[8,256]{1,0:T(8,128)S(1)} %dynamic_update_slice.3), channel_id=1, replica_groups=mesh['tm_0'=4,'tm_1'=8,'tm_2'=2,'series'=4] {'tm_0'}, use_global_device_ids=true, to_apply=%region_9.10 | all-reduce | flops 2048 | bytes 16384 | tf_op jit(solution)/shard_map/psum | solution.py:22
  132.1 13.5 %psum.29 = f32[8,256]{1,0:T(8,128)S(1)} all-reduce(f32[8,256]{1,0:T(8,128)S(1)} %psum.28), channel_id=1, replica_groups=mesh['tm_0'=4,'tm_1'=8,'tm_2'=2,'series'=4] {'tm_1'}, use_global_device_ids=true, to_apply=%region_10.11 | all-reduce | flops 2048 | bytes 16384 | tf_op jit(solution)/shard_map/psum | solution.py:22
  145.5 11.0 %psum.30 = f32[8,256]{1,0:T(8,128)S(1)} all-reduce(f32[8,256]{1,0:T(8,128)S(1)} %psum.29), channel_id=1, replica_groups=mesh['tm_0'=4,'tm_1'=8,'tm_2'=2,'series'=4] {'tm_2'}, use_global_device_ids=true, to_apply=%region_11.12 | all-reduce | flops 2048 | bytes 16384 | tf_op jit(solution)/shard_map/psum | solution.py:22
  156.5 7.0 %psum.31 = f32[8,256]{1,0:T(8,128)S(1)} all-reduce(f32[8,256]{1,0:T(8,128)S(1)} %psum.30), channel_id=1, replica_groups=mesh['tm_0'=4,'tm_1'=8,'tm_2'=2,'series'=4] {'series'}, use_global_device_ids=true, to_apply=%region_12.13 | all-reduce | flops 2048 | bytes 16384 | tf_op jit(solution)/shard_map/psum | solution.py:22
  163.5 0.7 constant_dynamic-slice_fusion
  (52 shorter events, 1.4 us)
Async XLA Ops:
  0.6 11.9 %copy-start.6 = (f32[8]{0:T(128)S(1)}, f32[8]{0:T(128)}, u32[]{:S(2)}) copy-start(f32[8]{0:T(128)} %param.3) | copy-start | bytes 100
  6.9 8.9 %collective-permute-start = (f32[256,8]{0,1:T(8,128)S(1)}, f32[256,8]{0,1:T(8,128)S(1)}, u32[]{:S(2)}, u32[]{:S(2)}) collective-permute-start(f32[256,8]{0,1:T(8,128)S(1)} %slice.70), channel_id=1, source_target_pairs={{0,1},{1,2},{2,3},{3,4},{4,5},{5,6},{6,7},{7,8},{8,9},{9,10},{10,1... | collective-permute-start | bytes 24584 | tf_op jit(solution)/shard_map/ppermute | solution.py:17
  12.0 61.9 %copy-start.8 = (s32[256]{0:T(256)}, s32[256]{0:T(256)S(1)}, u32[]{:S(2)}) copy-start(s32[256]{0:T(256)S(1)} %multiply_add_fusion.7) | copy-start | bytes 3076
  34.4 30.8 %all-to-all-start = ((f32[4,64,2048]{2,1,0:T(8,128)}), f32[4,64,2048]{2,1,0:T(8,128)S(1)}, u32[]{:S(2)}, u32[]{:S(2)}) async-start(f32[4,64,2048]{2,1,0:T(8,128)} %all_to_all.14), calls=%async_computation | async-start | bytes 4194304 | tf_op jit(solution)/shard_map/all_to_all | solution.py:68
  65.4 7.9 %collective-permute-start.1 = (f32[64,1024]{1,0:T(8,128)S(1)}, f32[64,1024]{1,0:T(8,128)S(1)}, u32[]{:S(2)}, u32[]{:S(2)}) collective-permute-start(f32[64,1024]{1,0:T(8,128)S(1)} %slice.72), channel_id=1, source_target_pairs={{0,4},{4,8},{8,12},{12,16},{16,20},{20,24},{24,28},{28,32},{32,36}... | collective-permute-start | bytes 786440 | tf_op jit(solution)/shard_map/ppermute | solution.py:17
  85.8 0.9 copy-start.9
  86.7 7.1 %copy-start.12 = (s32[128]{0:T(128)S(1)}, s32[128]{0:T(128)}, u32[]{:S(2)}) copy-start(s32[128]{0:T(128)} %multiply_add_fusion.13) | copy-start | bytes 1540
  93.7 6.3 %copy-start.11 = (s32[64]{0:T(128)S(1)}, s32[64]{0:T(128)}, u32[]{:S(2)}) copy-start(s32[64]{0:T(128)} %multiply_add_fusion.12) | copy-start | bytes 772
  105.9 0.7 copy-start.2
  105.9 0.7 copy-start
  105.9 0.8 copy-start.4
  106.0 6.5 %copy-start.1 = (f32[512]{0:T(512)S(1)}, f32[512]{0:T(512)}, u32[]{:S(2)}) copy-start(f32[512]{0:T(512)} %multiply_add_fusion.4) | copy-start | bytes 6148
  106.0 6.7 %copy-start.3 = (f32[256]{0:T(256)S(1)}, f32[256]{0:T(256)}, u32[]{:S(2)}) copy-start(f32[256]{0:T(256)} %multiply_add_fusion.5) | copy-start | bytes 3076
  106.1 6.8 %copy-start.7 = (s32[144]{0:T(256)S(1)}, s32[144]{0:T(256)}, u32[]{:S(2)}) copy-start(s32[144]{0:T(256)} %multiply_add_fusion.6) | copy-start | bytes 1732
  106.6 11.8 %copy-start.5 = (f32[128]{0:T(128)S(1)}, f32[128]{0:T(128)}, u32[]{:S(2)}) copy-start(f32[128]{0:T(128)} %multiply_add_fusion.9) | copy-start | bytes 1540
  106.6 12.0 %copy-start.10 = (f32[64]{0:T(128)S(1)}, f32[64]{0:T(128)}, u32[]{:S(2)}) copy-start(f32[64]{0:T(128)} %multiply_add_fusion.8) | copy-start | bytes 772
where the time goes:
time: 165 us; the launch traced here: 164 us
  matrix products  58.3 us (35%)
  blocking collectives  40.3 us (24%)
  waiting for transfers between devices  23.6 us (14%)
  local copies, waits for them, and re-layouts  17.4 us (11%)
  starting transfers between devices  13.3 us (8%)
  other arithmetic  9.51 us (6%)
  between operations  1.76 us (1%)
    dot_general x8, matrix products, decimate(): jnp.einsum('rbi,io->rbo', extended, table, precision=lax.Precision.HIGHEST)  58.3 us
    psum x4, blocking collectives, by_axis(): shard = lax.psum(shard, axis)  40.3 us
    all_to_all x1, waiting for transfers between devices, body(): lax.all_to_all(first, 'series', split_axis=0, concat_axis=1, tiled=True)  21.8 us
    ppermute x2, starting transfers between devices, shifted(): return lax.ppermute(block, axis, route)  8.7 us
    unnamed x27, local copies, waits for them, and re-layouts  5.93 us
    all_to_all x1, starting transfers between devices, body(): lax.all_to_all(first, 'series', split_axis=0, concat_axis=1, tiled=True)  4.65 us
  transfers between devices with their start and end apart: 3, of which 2 were waited for; matrix products, arithmetic and copies ran while one was open for 6% of the time, Pallas kernels for 0%

commit v1 on v0

v1 whole, which is shorter than its diff:
```python
import functools
import math

import jax
import jax.numpy as jnp
from jax import lax
from jax.experimental import pallas as pl
from jax.experimental.pallas import tpu as pltpu
from jax.sharding import PartitionSpec as P

LEVELS = 8
TAPS = 8
BLOCK = 256
BLOCKS = 16
SLAB = 64
N_Y, N_Z, N_CORE, N_X = 4, 8, 2, 4
TIME = 1048576
MESH = pl.DeviceIdType.MESH
F32 = jnp.float32
BF16 = jnp.bfloat16


def lanes(rows):
    return lax.broadcasted_iota(jnp.int32, (rows, 128), 1)


def sublanes(rows):
    return lax.broadcasted_iota(jnp.int32, (rows, 128), 0)


def checksum_weights(rows, level, first_block, group):
    lane = lanes(rows)
    block = first_block + 8 * group + lax.rem(lane, 64) // 8
    count = TIME >> level
    at = sublanes(rows) + block * (BLOCK >> level)
    weight = (1.0 + (2.0 / (count - 1)) * at.astype(F32)) * (1.0 / math.sqrt(count))
    keep = (lax.rem(lane, 8) == level - 1) & (at < count)
    return jnp.where(keep, weight, 0.0)


def build_table(taps_ref, pull, table, first_block):
    total = taps_ref[0]
    for t in range(1, TAPS):
        total = total + taps_ref[t]
    scale = math.sqrt(2.0) / jnp.full((1, 128), total, F32)
    kernel = [scale * taps_ref[t] for t in range(TAPS)]

    lane8, row8 = lanes(8), sublanes(8)
    pull[0, 0, 0:8] = jnp.where((lax.rem(lane8, 64) == row8) & (row8 < 7), 1.0, 0.0)
    for g in range(2):
        pull[0, 1 + g, 0:8] = jnp.where(
            row8 < 7, checksum_weights(8, LEVELS, first_block, g), 0.0
        )
    for level in range(LEVELS, 0, -1):
        src, dst = (LEVELS - level) % 2, (LEVELS - level + 1) % 2
        half = (BLOCK >> level) + 3 if level > 1 else BLOCK // 2
        for a in range(3):
            parts = [pull[src, a, pl.ds(s, half)] for s in range(4)]
            for parity in range(2):
                out = parts[0] * kernel[1 - parity]
                for s in range(1, 4):
                    out = out + parts[s] * kernel[2 * s + 1 - parity]
                pull[dst, a, pl.ds(parity, half, stride=2)] = out
        if level > 1:
            rows = (BLOCK >> (level - 1)) + 6
            for g in range(2):
                pull[dst, 1 + g, 0:rows] += checksum_weights(rows, level - 1, first_block, g)

    lane = lanes(BLOCK)
    split = []
    for a in range(3):
        value = pull[0, a, 0:BLOCK]
        high = value.astype(BF16).astype(F32)
        split.append(jnp.where(lane < 64, high, value - high))
    coarse_lane = lax.rem(lane, 64) < 24
    for b in range(BLOCKS):
        shift = (24 - 8 * (b % 8)) % 128
        own = split[0] if b == 0 else pltpu.roll(split[0], b, 1)
        sums = split[1 + b // 8]
        if shift:
            sums = pltpu.roll(sums, shift, 1)
        table[b] = jnp.where(coarse_lane, own, sums).astype(BF16)


def reduce_slab(x_ref, table):
    total = jnp.zeros((2 * SLAB, 128), F32)
    for b in range(BLOCKS):
        x = x_ref[:, pl.ds(BLOCK * b, BLOCK)]
        high = x.astype(BF16)
        low = (x - high.astype(F32)).astype(BF16)
        total += jnp.dot(
            jnp.concatenate([high, low], axis=0), table[b], preferred_element_type=F32
        )
    y = total[:SLAB] + total[SLAB:]
    return y + pltpu.roll(y, 64, 1)


def pack_slab(y):
    lane = lanes(16)
    packed = y[0:16]
    for g in range(1, 4):
        packed = jnp.where(lane // 32 == g, pltpu.roll(y[16 * g : 16 * g + 16], 32 * g, 1), packed)
    turned = jnp.concatenate([y, y], axis=0).T
    return packed, turned[24:32]


def body_kernel(
    taps_ref, x_ref, coarse_ref, sums_ref,
    x_buf, pull, table, outbox, inbox, spill, mid, far, mine2,
    x_sem, send1, recv1, send_s, recv_s, send2, recv2, send3, recv3,
):
    tm, s = lax.axis_index("tm"), lax.axis_index("series")
    core, z, y = tm % N_CORE, (tm // N_CORE) % N_Z, tm // (N_CORE * N_Z)
    n_tm = N_Y * N_Z * N_CORE
    order = (2, 1, 3, 0)

    def loads(k):
        slab = (s + k) % N_X
        return pltpu.make_async_copy(
            x_ref.at[pl.ds(pl.multiple_of(slab * SLAB, SLAB), SLAB)], x_buf.at[k], x_sem.at[k]
        )

    for k in order:
        loads(k).start()

    next_tm, last_tm = (tm + 1) % n_tm, (tm + n_tm - 1) % n_tm
    near = [(dy, dc) for dy in range(N_Y) for dc in range(N_CORE) if dy or dc]

    def near_tm(dy, dc):
        return (((y + dy) % N_Y) * N_Z + z) * N_CORE + (core + dc) % N_CORE

    def far_tm(dz):
        return (y * N_Z + (z + dz) % N_Z) * N_CORE + core

    barrier = pltpu.get_barrier_semaphore()

    def greet(t, r):
        pl.semaphore_signal(barrier, inc=1, device_id=(t, r), device_id_type=MESH)

    for dz in range(1, N_Z):
        greet(far_tm(dz), s)
    for dy, dc in near:
        greet(near_tm(dy, dc), s)
    for k in range(1, N_X):
        greet(tm, (s + k) % N_X)
    greet(last_tm, N_X - 1)

    @pl.when(s == N_X - 1)
    def _():
        for r in range(N_X):
            greet(next_tm, r)

    build_table(taps_ref, pull, table, BLOCKS * (N_X * tm + s))

    def exchange(k):
        slab = (s + k) % N_X
        return pltpu.make_async_remote_copy(
            src_ref=outbox.at[k], dst_ref=inbox.at[s],
            send_sem=send1.at[k], recv_sem=recv1.at[k],
            device_id=(tm, slab), device_id_type=MESH,
        )

    def hand_on(k):
        slab = (s + k) % N_X
        return pltpu.make_async_remote_copy(
            src_ref=outbox.at[k, 0:16], dst_ref=spill,
            send_sem=send_s.at[k], recv_sem=recv_s,
            device_id=(next_tm, slab), device_id_type=MESH,
        )

    for k in order:
        loads(k).wait()
        packed, turned = pack_slab(reduce_slab(x_buf.at[k], table))
        outbox[k, 0:16] = packed
        outbox[k, 16:24] = turned
        if k == 2:
            pl.semaphore_wait(barrier, 18 + N_X * (s // (N_X - 1)))

        if k:
            exchange(k).start()
        else:
            inbox[s] = outbox[0]

        @pl.when(s == N_X - 1)
        def _():
            hand_on(k).start()

    for k in range(1, N_X):
        exchange(k).wait_recv()
    part = inbox[0, 16:24]
    for r in range(1, N_X):
        part += inbox[r, 16:24]

    q = y * N_CORE + core
    mine2[0] = part
    mid[q] = part

    def near_copy(i):
        dy, dc = near[i]
        return pltpu.make_async_remote_copy(
            src_ref=mine2.at[0], dst_ref=mid.at[q],
            send_sem=send2.at[i], recv_sem=recv2.at[i],
            device_id=(near_tm(dy, dc), s), device_id_type=MESH,
        )

    for i in range(len(near)):
        near_copy(i).start()

    hand_on(0).wait_recv()
    lane = lanes(16)
    for g in range(4):
        out = jnp.zeros((16, 128), F32)
        for r in range(N_X):
            value = inbox[r, 0:16]
            shift = (16 * r - 32 * g) % 128
            if shift:
                value = pltpu.roll(value, shift, 1)
            out += jnp.where((lane >= 16 * r) & (lane < 16 * r + 22), value, 0.0)
        value = pltpu.roll(spill[...], (-16 - 32 * g) % 128, 1)
        out += jnp.where((lane < 6) & (tm > 0), value, 0.0)
        coarse_ref[pl.ds(16 * g, 16), :] = out[:, 0:64]

    for i in range(len(near)):
        near_copy(i).wait_recv()
    part = mid[0]
    for i in range(1, N_Y * N_CORE):
        part += mid[i]
    mine2[1] = part
    far[z] = part

    def far_copy(dz):
        return pltpu.make_async_remote_copy(
            src_ref=mine2.at[1], dst_ref=far.at[z],
            send_sem=send3.at[dz], recv_sem=recv3.at[dz],
            device_id=(far_tm(dz), s), device_id_type=MESH,
        )

    for dz in (4, 3, 5, 2, 6, 1, 7):
        far_copy(dz).start()
    for k in range(1, N_X):
        exchange(k).wait_send()

    @pl.when(s == N_X - 1)
    def _():
        for k in range(N_X):
            hand_on(k).wait_send()

    for i in range(len(near)):
        near_copy(i).wait_send()
    for dz in range(1, N_Z):
        far_copy(dz).wait_recv()
    part = far[0]
    for i in range(1, N_Z):
        part += far[i]
    sums_ref[...] = part[:, 0:64]
    for dz in range(1, N_Z):
        far_copy(dz).wait_send()


def body(samples, taps):
    vmem = functools.partial(pltpu.VMEM)
    dma = pltpu.SemaphoreType.DMA
    return pl.pallas_call(
        body_kernel,
        out_shape=(
            jax.ShapeDtypeStruct((SLAB, 64), F32),
            jax.ShapeDtypeStruct((LEVELS, SLAB), F32),
        ),
        in_specs=[
            pl.BlockSpec(memory_space=pltpu.SMEM),
            pl.BlockSpec(memory_space=pl.ANY),
        ],
        out_specs=(
            pl.BlockSpec(memory_space=pltpu.VMEM),
            pl.BlockSpec(memory_space=pltpu.VMEM),
        ),
        scratch_shapes=[
            vmem((N_X, SLAB, BLOCK * BLOCKS), F32),
            vmem((2, 3, 272, 128), F32),
            vmem((BLOCKS, BLOCK, 128), BF16),
            vmem((N_X, 24, 128), F32),
            vmem((N_X, 24, 128), F32),
            vmem((16, 128), F32),
            vmem((8, 8, 128), F32),
            vmem((8, 8, 128), F32),
            vmem((2, 8, 128), F32),
            dma((N_X,)),
            dma((N_X,)),
            dma((N_X,)),
            dma((N_X,)),
            dma(()),
            dma((7,)),
            dma((7,)),
            dma((8,)),
            dma((8,)),
        ],
        compiler_params=pltpu.CompilerParams(collective_id=0, has_side_effects=True),
        name="rollup",
    )(taps, samples)


def solution(mesh):
    return jax.shard_map(
        body,
        mesh=mesh,
        in_specs=(P(None, ("tm", "series")), P()),
        out_specs=(P("series", "tm"), P(None, "series")),
        check_vma=False,
    )
```

time: 165 us -> 26.6 us (0.16)
  matrix products: 58.3 us -> 0 us
  blocking collectives: 40.3 us -> 0 us
  waiting for transfers between devices: 23.6 us -> 0 us
  Pallas kernels: 0 us -> 23.1 us
  local copies, waits for them, and re-layouts: 17.4 us -> 2.65 us
  starting transfers between devices: 13.3 us -> 0 us
  other arithmetic: 9.51 us -> 0 us
    dot_general x8 -> x0, matrix products: 58.3 us -> none  [decimate(): jnp.einsum('rbi,io->rbo', extended, table, precision=lax.Precision.HIGHEST)]
    psum x4 -> x0, blocking collectives: 40.3 us -> none  [by_axis(): shard = lax.psum(shard, axis)]
    pallas_call x0 -> x1, Pallas kernels: none -> 23.1 us  [body(): pl.pallas_call(body_kernel, out_shape=(jax.ShapeDtypeStruct((SLAB, 64), F...]
    all_to_all x1 -> x0, waiting for transfers between devices: 21.8 us -> none  [body(): lax.all_to_all(first, 'series', split_axis=0, concat_axis=1, tiled=True)]
    ppermute x2 -> x0, starting transfers between devices: 8.7 us -> none  [shifted(): return lax.ppermute(block, axis, route)]
    add x15 -> x0, other arithmetic: 6.96 us -> none  [the longest x8 2.91 us: level_sums(): weights_pos = 1.0 + 2.0 * position / (global_len - 1)]
    all_to_all x1 -> x0, starting transfers between devices: 4.65 us -> none  [body(): lax.all_to_all(first, 'series', split_axis=0, concat_axis=1, tiled=True)]
    unnamed x27 -> x2, local copies, waits for them, and re-layouts: 5.93 us -> 2.65 us
  transfers between devices with their start and end apart: 3 -> 0, of which waited for: 2 -> 0; matrix products, arithmetic and copies ran while one was open for 6% -> 0% of each run, Pallas kernels for 0% -> 0%
where the time goes in v1:
time: 26.6 us; the launch traced here: 26.4 us
  Pallas kernels  23.1 us (87%)
  local copies, waits for them, and re-layouts  2.65 us (10%)
  between operations  0.64 us (2%)
    pallas_call x1, Pallas kernels, body(): pl.pallas_call(body_kernel, out_shape=(jax.ShapeDtypeStruct((SLAB, 64), F...  23.1 us
    unnamed x2, local copies, waits for them, and re-layouts  2.65 us

profile of v1, /device:TPU:1, one launch (start us, length us, event | category | flops | bytes accessed | tf_op | source)
XLA Modules:
  0.0 26.4 jit_solution(7659086187831348429)
XLA Ops:
  0.6 23.1 %rollup.1 = (f32[64,64]{1,0:T(8,128)}, f32[8,64]{1,0:T(8,128)}) custom-call(f32[8]{0:T(128)} %taps_ref.1, f32[256,4096]{1,0:T(8,128)} %x_ref.1), custom_call_target="tpu_custom_call" | custom-call | tf_op jit(solution)/shard_map/rollup/pallas_call | solution.py:263
  23.8 1.4 %copy.6 = f32[64,64]{1,0:T(8,128)} copy(f32[64,64]{1,0:T(8,128)} %get-tuple-element.4) | data formatting | bytes 32768
  25.1 1.3 %copy.7 = f32[8,64]{1,0:T(8,128)} copy(f32[8,64]{1,0:T(8,128)} %get-tuple-element.5) | data formatting | bytes 4096

commit v2 on v1

v2 whole, which is shorter than its diff:
```python
import math

import jax
import jax.numpy as jnp
from jax import lax
from jax.experimental import pallas as pl
from jax.experimental.pallas import tpu as pltpu
from jax.sharding import PartitionSpec as P

LEVELS = 8
TAPS = 8
BLOCK = 256
BLOCKS = 16
SLAB = 64
N_Y, N_Z, N_CORE, N_X = 4, 8, 2, 4
N_TM = N_Y * N_Z * N_CORE
TIME = 1048576
LAST_BLOCK = TIME // BLOCK
ORDER = (2, 1, 3, 0)
MESH = pl.DeviceIdType.MESH
F32 = jnp.float32
BF16 = jnp.bfloat16


def lanes(rows):
    return lax.broadcasted_iota(jnp.int32, (rows, 128), 1)


def sublanes(rows):
    return lax.broadcasted_iota(jnp.int32, (rows, 128), 0)


def seed_rows(level):
    return (BLOCK >> level) + 6


def seeds(level):
    rows = -(-seed_rows(level) // 8) * 8
    lane, row = lanes(rows), sublanes(rows)
    count, step = TIME >> level, BLOCK >> level
    slope, scale = 2.0 / (count - 1), 1.0 / math.sqrt(count)
    group = lane // 8
    mine = (lane % 8 == level - 1) & (row < seed_rows(level))
    back = group - 4
    past = (back >= 1) & (back <= 6) & (row >= back * step)
    at = row + jnp.where(back >= 1, step * (LAST_BLOCK - back), 0)
    value = (1.0 + slope * at.astype(F32)) * scale
    value = jnp.where(mine & ((group == 3) | past), value, 0.0)
    value = jnp.where(mine & (group == 4), slope * step * scale, value)
    if level == LEVELS:
        value = jnp.where((lane == row) & (row < 7), 1.0, value)
    return value


def build_table(taps_ref, seed, pull, table):
    total = taps_ref[0]
    for t in range(1, TAPS):
        total = total + taps_ref[t]
    scale = math.sqrt(2.0) / jnp.full((1, 128), total, F32)
    kernel = [scale * taps_ref[t] for t in range(TAPS)]

    for level in range(LEVELS, 0, -1):
        src = seed if level == LEVELS else pull
        first, into = (0, 0) if level == LEVELS else ((LEVELS - level - 1) % 2, (LEVELS - level) % 2)
        half = (BLOCK >> level) + 3 if level > 1 else BLOCK // 2
        parts = [src[first, pl.ds(s, half)] for s in range(4)]
        for parity in range(2):
            out = parts[0] * kernel[1 - parity]
            for s in range(1, 4):
                out = out + parts[s] * kernel[2 * s + 1 - parity]
            if level > 1:
                out = out + seed[LEVELS - level + 1, pl.ds(parity, half, stride=2)]
            pull[into, pl.ds(parity, half, stride=2)] = out

    value = pull[1, 0:BLOCK]
    high = value.astype(BF16)
    table[:, 0:128] = high
    table[:, 128:256] = (value - high.astype(F32)).astype(BF16)


def multiply(x_ref, accs):
    for b in range(BLOCKS):
        x = x_ref[:, pl.ds(BLOCK * b, BLOCK)]
        high = x.astype(BF16)
        pltpu.matmul_acc_lhs(accs[b], high)
        pltpu.matmul_acc_lhs(accs[b], x - high.astype(F32))


def finish(accs, first_block, at_end):
    spread = jnp.zeros((SLAB, 128), F32)
    plain = jnp.zeros((SLAB, 128), F32)
    slanted = jnp.zeros((SLAB, 128), F32)
    over = jnp.zeros((SLAB, 128), F32)
    for b in range(BLOCKS):
        y = pltpu.matmul_pop(accs[b])
        y = y[:, 0:128] + y[:, 128:256]
        spread += pltpu.roll(y, b, 1) if b else y
        plain += y
        if b < BLOCKS - 1:
            slanted += plain
        back = BLOCKS - b
        if back <= 6:
            over += pltpu.roll(y, 128 - 8 * (back + 1), 1)
    lifted = plain * (first_block + (BLOCKS - 1)) - slanted
    sums = plain + pltpu.roll(lifted, 120, 1) - at_end * over
    spread = jnp.where(lanes(SLAB) < 24, spread, 0.0)
    packed = spread[0:16]
    for g in range(1, 4):
        packed += pltpu.roll(spread[16 * g : 16 * g + 16], 32 * g, 1)
    turned = jnp.concatenate([sums, sums], axis=0).T
    return packed, turned[24:32]


def body_kernel(
    taps_hbm, x_hbm, coarse_ref, sums_ref,
    taps_ref, x_buf, seed, pull, table,
    outbox, inbox, spill, outsum, insum, mine, far,
    taps_sem, x_sem, send1, recv1, send_s, recv_s, send2, recv2, send3, send4, recv3,
):
    def scoped(*accs):
        kernel_body(
            taps_hbm, x_hbm, coarse_ref, sums_ref,
            taps_ref, x_buf, seed, pull, table,
            outbox, inbox, spill, outsum, insum, mine, far,
            taps_sem, x_sem, send1, recv1, send_s, recv_s, send2, recv2, send3, send4, recv3,
            (accs[:BLOCKS], accs[BLOCKS:]),
        )

    pl.run_scoped(
        scoped, *[pltpu.ACC(b % 2)((SLAB, 256), F32) for _ in range(2) for b in range(BLOCKS)]
    )


def kernel_body(
    taps_hbm, x_hbm, coarse_ref, sums_ref,
    taps_ref, x_buf, seed, pull, table,
    outbox, inbox, spill, outsum, insum, mine, far,
    taps_sem, x_sem, send1, recv1, send_s, recv_s, send2, recv2, send3, send4, recv3,
    accs,
):
    tm, s = lax.axis_index("tm"), lax.axis_index("series")
    core, z, y = tm % N_CORE, (tm // N_CORE) % N_Z, tm // (N_CORE * N_Z)
    next_tm, last_tm = (tm + 1) % N_TM, (tm + N_TM - 1) % N_TM

    taps_load = pltpu.make_async_copy(taps_hbm, taps_ref, taps_sem)
    taps_load.start()

    def load(k):
        slab = (s + k) % N_X
        return pltpu.make_async_copy(
            x_hbm.at[pl.ds(pl.multiple_of(slab * SLAB, SLAB), SLAB)], x_buf.at[k], x_sem.at[k]
        )

    for k in ORDER:
        load(k).start()

    def plane(dy, c):
        return (((y + dy) % N_Y) * N_Z + z) * N_CORE + c

    def column(dz, c):
        return (y * N_Z + (z + dz) % N_Z) * N_CORE + c

    barrier = pltpu.get_barrier_semaphore()

    def greet(t, r):
        pl.semaphore_signal(barrier, inc=1, device_id=(t, r), device_id_type=MESH)

    for dz in (4, 3, 5, 2, 6, 1, 7):
        greet(column(dz, 1), s)
    for dx in (2, 1, 3, 0):
        for dy in (2, 1, 3, 0):
            if dx or dy:
                greet(plane(dy, 1), (s + dx) % N_X)
    greet(last_tm, N_X - 1)

    @pl.when(core == 0)
    def _():
        greet(tm + 1, s)
        for dx in range(1, N_X):
            greet(tm, (s + dx) % N_X)

    @pl.when(core == 1)
    def _():
        for dz in (4, 3, 5, 2, 6, 1, 7):
            greet(column(dz, 0), s)
        for dx in (2, 1, 3, 0):
            for dy in (2, 1, 3, 0):
                greet(plane(dy, 0), (s + dx) % N_X)

    @pl.when(s == N_X - 1)
    def _():
        for r in range(N_X):
            greet(next_tm, r)

    greetings = 27 + 19 * core + N_X * (s // (N_X - 1))

    for level in range(LEVELS, 0, -1):
        value = seeds(level)
        seed[LEVELS - level, 0 : value.shape[0]] = value
    taps_load.wait()
    build_table(taps_ref, seed, pull, table)
    for q in range(2):
        pltpu.matmul_push_rhs(table[...], staging_register=0, mxu_index=q)
        pltpu.matmul_acc_lhs(accs[1][q], jnp.zeros((SLAB, 256), BF16), load_staged_rhs=0)

    first_block = (BLOCKS * (N_X * tm + s)).astype(F32)
    at_end = ((tm * N_X + s) // (N_TM * N_X - 1)).astype(F32)

    def exchange(k):
        return pltpu.make_async_remote_copy(
            src_ref=outbox.at[k], dst_ref=inbox.at[s],
            send_sem=send1.at[k], recv_sem=recv1.at[k],
            device_id=(tm, (s + k) % N_X), device_id_type=MESH,
        )

    def hand_on(k):
        return pltpu.make_async_remote_copy(
            src_ref=outbox.at[k], dst_ref=spill,
            send_sem=send_s.at[k], recv_sem=recv_s,
            device_id=(next_tm, (s + k) % N_X), device_id_type=MESH,
        )

    def gather(k, dy, c=None):
        at = (s * N_Y + y) * N_CORE + core
        return pltpu.make_async_remote_copy(
            src_ref=outsum.at[k], dst_ref=insum.at[at],
            send_sem=send2.at[k * N_Y + dy],
            recv_sem=recv2.at[(k * N_Y + dy) * N_CORE + (core if c is None else c)],
            device_id=(plane(dy, 1), (s + k) % N_X), device_id_type=MESH,
        )

    def ship(k):
        packed, turned = finish(accs[ORDER.index(k) % 2], first_block, at_end)
        outsum[k] = turned
        outbox[k] = packed
        if k == ORDER[0]:
            pl.semaphore_wait(barrier, greetings)
        for dy in (2, 1, 3, 0):
            if k or dy:
                gather(k, dy).start()
        if k:
            exchange(k).start()
        else:
            insum[(s * N_Y + y) * N_CORE + core] = turned
            inbox[s] = packed

            @pl.when(core == 0)
            def _():
                gather(0, 0).start()

        @pl.when(s == N_X - 1)
        def _():
            hand_on(k).start()

    for i, k in enumerate(ORDER):
        load(k).wait()
        multiply(x_buf.at[k], accs[i % 2])
        if i:
            ship(ORDER[i - 1])
    ship(ORDER[-1])

    def across(dz, c, sems):
        return pltpu.make_async_remote_copy(
            src_ref=mine, dst_ref=far.at[z],
            send_sem=sems.at[dz], recv_sem=recv3.at[dz],
            device_id=(column(dz, c), s), device_id_type=MESH,
        )

    @pl.when(core == 1)
    def _():
        for k in range(N_X):
            for dy in range(N_Y):
                for c in range(N_CORE):
                    if k or dy or not c:
                        gather(k, dy, c).wait_recv()
        part = insum[0]
        for i in range(1, N_X * N_Y * N_CORE):
            part += insum[i]
        mine[...] = part
        far[z] = part
        for dz in (4, 3, 5, 2, 6, 1, 7):
            across(dz, 0, send4).start()
            across(dz, 1, send3).start()
        across(0, 0, send4).start()

    for k in range(1, N_X):
        exchange(k).wait_recv()
    hand_on(0).wait_recv()
    lane = lanes(16)
    for g in range(4):
        out = jnp.zeros((16, 128), F32)
        for r in range(N_X):
            value = inbox[r]
            shift = (16 * r - 32 * g) % 128
            if shift:
                value = pltpu.roll(value, shift, 1)
            out += jnp.where((lane >= 16 * r) & (lane < 16 * r + 22), value, 0.0)
        value = pltpu.roll(spill[...], (-16 - 32 * g) % 128, 1)
        out += jnp.where((lane < 6) & (tm > 0), value, 0.0)
        coarse_ref[pl.ds(16 * g, 16), :] = out[:, 0:64]

    for k in range(N_X):
        for dy in range(N_Y):
            if k or dy:
                gather(k, dy).wait_send()
        if k:
            exchange(k).wait_send()

    @pl.when(core == 0)
    def _():
        gather(0, 0).wait_send()

    @pl.when(s == N_X - 1)
    def _():
        for k in range(N_X):
            hand_on(k).wait_send()

    @pl.when(core == 0)
    def _():
        across(0, 0, send4).wait_recv()

    for dz in range(1, N_Z):
        across(dz, 0, send4).wait_recv()
    part = far[0]
    for i in range(1, N_Z):
        part += far[i]
    sums_ref[...] = part[:, 0:64]

    @pl.when(core == 1)
    def _():
        across(0, 0, send4).wait_send()
        for dz in range(1, N_Z):
            across(dz, 0, send4).wait_send()
            across(dz, 1, send3).wait_send()


def hand_out(coarse_ref, sums_ref, coarse_out, sums_out):
    coarse_out[...] = coarse_ref[...]
    sums_out[...] = sums_ref[...]


def body(samples, taps):
    vmem, dma = pltpu.VMEM, pltpu.SemaphoreType.DMA
    on_chip = pl.BlockSpec(memory_space=pltpu.VMEM)
    shapes = ((SLAB, 64), (LEVELS, SLAB))
    coarse, sums = pl.pallas_call(
        body_kernel,
        out_shape=tuple(vmem(shape, F32) for shape in shapes),
        in_specs=[pl.BlockSpec(memory_space=pl.ANY)] * 2,
        out_specs=(on_chip, on_chip),
        scratch_shapes=[
            pltpu.SMEM((TAPS,), F32),
            vmem((N_X, SLAB, BLOCK * BLOCKS), F32),
            vmem((LEVELS, 136, 128), F32),
            vmem((2, 256, 128), F32),
            vmem((BLOCK, 256), BF16),
            vmem((N_X, 16, 128), F32),
            vmem((N_X, 16, 128), F32),
            vmem((16, 128), F32),
            vmem((N_X, 8, 128), F32),
            vmem((N_X * N_Y * N_CORE, 8, 128), F32),
            vmem((8, 128), F32),
            vmem((N_Z, 8, 128), F32),
            dma(()),
            dma((N_X,)),
            dma((N_X,)),
            dma((N_X,)),
            dma((N_X,)),
            dma(()),
            dma((N_X * N_Y,)),
            dma((N_X * N_Y * N_CORE,)),
            dma((N_Z,)),
            dma((N_Z,)),
            dma((N_Z,)),
        ],
        compiler_params=pltpu.CompilerParams(collective_id=0, has_side_effects=True),
        name="rollup",
    )(taps, samples)
    return pl.pallas_call(
        hand_out,
        out_shape=tuple(jax.ShapeDtypeStruct(shape, F32) for shape in shapes),
        in_specs=[on_chip, on_chip],
        out_specs=(on_chip, on_chip),
        name="hand_out",
    )(*(pltpu.with_memory_space_constraint(v, pltpu.VMEM) for v in (coarse, sums)))


def solution(mesh):
    return jax.shard_map(
        body,
        mesh=mesh,
        in_specs=(P(None, ("tm", "series")), P()),
        out_specs=(P("series", "tm"), P(None, "series")),
        check_vma=False,
    )
```

time: 26.6 us -> 20.9 us (0.79)
  Pallas kernels: 23.1 us -> 20.2 us
  local copies, waits for them, and re-layouts: 2.65 us -> 0 us
    pallas_call x1 -> x2, Pallas kernels: 23.1 us -> 20.2 us  [the longest x1 19.6 us: body(): pl.pallas_call(body_kernel, out_shape=tuple((vmem(shape, F32) for shape i...]
    unnamed x2 -> x0, local copies, waits for them, and re-layouts: 2.65 us -> none
where the time goes in v2:
time: 20.9 us; the launch traced here: 20.8 us
  Pallas kernels  20.2 us (97%)
  between operations  0.64 us (3%)
    pallas_call x1, Pallas kernels, body(): pl.pallas_call(body_kernel, out_shape=tuple((vmem(shape, F32) for shape i...  19.6 us
    pallas_call x1, Pallas kernels, body(): pl.pallas_call(hand_out, out_shape=tuple((jax.ShapeDtypeStruct(shape, F32...  0.62 us

profile of v2, /device:TPU:1, one launch (start us, length us, event | category | flops | bytes accessed | tf_op | source)
XLA Modules:
  0.0 20.8 jit_solution(1748643578597931706)
XLA Ops:
  0.6 19.6 %rollup.1 = (f32[64,64]{1,0:T(8,128)S(1)}, f32[8,64]{1,0:T(8,128)S(1)}) custom-call(f32[8]{0:T(128)} %taps_hbm.1, f32[256,4096]{1,0:T(8,128)} %x_hbm.1), custom_call_target="tpu_custom_call" | custom-call | tf_op jit(solution)/shard_map/rollup/pallas_call | solution.py:346
  20.2 0.6 %hand_out.1 = (f32[64,64]{1,0:T(8,128)}, f32[8,64]{1,0:T(8,128)}) custom-call(f32[64,64]{1,0:T(8,128)S(1)} %get-tuple-element.4.coarse_ref, f32[8,64]{1,0:T(8,128)S(1)} %get-tuple-element.5.sums_ref), custom_call_target="tpu_custom_call" | custom-call | tf_op jit(solution)/shard_map/hand_out/pallas_call | solution.py:379
